TPU v7x, 32 devices: a whole 2x2x4 slice. The times are simulated.
32 devices in a mesh: layer: 4 (over z), leaf: 8 (over y, x, core).
Axes of the slice: x: 2, y: 2, z: 4, core: 2. Of those that a mesh axis runs over, the one named last changes fastest.
Arguments:
- right_side: bfloat16 [4, 2, 32, 8192], P('layer', None, None, 'leaf'), may hold values from -6 to 6
- near_blocks: bfloat16 [4, 3, 2, 8192, 256], P('layer', None, None, 'leaf'), may hold values from -0.21875 to 0.21875
- right_bases: bfloat16 [4, 2, 2, 16, 8192], P('layer', None, None, None, 'leaf'), may hold values from -0.125 to 0.125
- left_bases: bfloat16 [4, 2, 2, 16, 8192], P('layer', None, None, None, 'leaf'), may hold values from -1 to 1
- coupling: bfloat16 [4, 8192], P('layer', 'leaf'), may hold values from 0.25 to 0.69921875
- ranks: int32 [4, 6], P('layer'), may hold values from 8 to 16
Outputs:
- swept: bfloat16 [4, 2, 32, 8192], P('layer', None, None, 'leaf')
Inputs may be any that keep to these rules, and one draw needn't show every extreme that they name: ranks[k, s] is the rank in use of layer k's far block that maps into cluster s at level 0 (s = 0, 1) or cluster s - 2 at level 1 (s = 2 to 5).
All inputs are finite; a program needn't handle non-finite values.
Results may differ from a plain program's by a relative error of at most 0.035.
Values may be sent and summed in bfloat16 or wider, within the bound.
A program may use at most 64 MiB of HBM per device.

v0:
```python
import functools

import jax
import jax.numpy as jnp
from jax import lax
from jax.experimental import pallas as pl
from jax.experimental.pallas import tpu as pltpu
from jax.sharding import PartitionSpec as P

BATCHES = 2
SUM_TYPE = jnp.bfloat16
F32 = jnp.float32
BF16 = jnp.bfloat16
LANES = (((1,), (1,)), ((), ()))


def kernel(
    layers, leafs, batches,
    source_hbm, near_hbm, right_hbm, left_hbm, coupling_ref, ranks_ref,
    out_ref,
    source, near, right, right_next, left_raw, left, inner,
    rim, part, part_sent, moved, sent, moved_rim, moved_part, moved_part_sent,
    load_sem, near_sem, rim_sem, part_sem, right_sem, move_sem, move_rim_sem, move_part_sem,
):
    layer = lax.axis_index("layer")
    leaf = lax.axis_index("leaf")
    rows, width = source.shape[1], source.shape[2]
    cells = near.shape[-1]
    count = width // cells
    rank = right.shape[2]
    group = rows // batches
    half, quarter = leafs // 2, leafs // 4
    upper, lower = leaf // half, leaf // quarter
    has_low, has_high = leaf > 0, leaf < leafs - 1
    odd, even = lax.rem(leaf, 2) == 1, lax.rem(leaf, 2) == 0
    has_prev, has_next = layer > 0, layer < layers - 1

    def remote(src, dst, sems, index, to_layer, to_leaf, landing=None):
        return pltpu.make_async_remote_copy(
            src_ref=src, dst_ref=dst,
            send_sem=sems.at[(0,) + index],
            recv_sem=sems.at[(1,) + (index if landing is None else landing)],
            device_id=(to_layer, to_leaf), device_id_type=pl.DeviceIdType.MESH,
        )

    loads = [
        pltpu.make_async_copy(source_hbm.at[0], source, load_sem.at[0]),
        pltpu.make_async_copy(right_hbm.at[0], right, load_sem.at[1]),
        pltpu.make_async_copy(left_hbm.at[0], left_raw, load_sem.at[2]),
    ]
    near_loads = [
        pltpu.make_async_copy(
            near_hbm.at[0, :, :, pl.ds(q * cells, cells), :], near.at[q], near_sem.at[q]
        )
        for q in range(count)
    ]
    order = list(range(1, count - 1)) + ([0, count - 1] if count > 1 else [0])
    for copy in loads:
        copy.start()
    for q in order:
        near_loads[q].start()

    barrier = pltpu.get_barrier_semaphore()

    def greet(to_layer, to_leaf):
        pl.semaphore_signal(
            barrier, inc=1, device_id=(to_layer, to_leaf), device_id_type=pl.DeviceIdType.MESH
        )

    for step in range(1, leafs):
        greet(layer, lax.rem(leaf + step, leafs))

    @pl.when(has_prev)
    def _():
        for other in range(leafs):
            greet(layer - 1, other)

    @pl.when(has_next)
    def _():
        for other in range(leafs):
            greet(layer + 1, other)

    @pl.when(jnp.logical_not(has_low))
    def _():
        rim[0] = jnp.zeros(rim.shape[1:], BF16)
        for b in range(batches):
            moved_rim[b, 0] = jnp.zeros(moved_rim.shape[2:], BF16)

    @pl.when(jnp.logical_not(has_high))
    def _():
        rim[1] = jnp.zeros(rim.shape[1:], BF16)
        for b in range(batches):
            moved_rim[b, 1] = jnp.zeros(moved_rim.shape[2:], BF16)

    def stacked(real, imag):
        return jnp.concatenate([real, imag], axis=0), jnp.concatenate([-imag, real], axis=0)

    def partial_sums(first, second, bases):
        flat = jnp.concatenate(
            [bases[:, 0].reshape(2 * rank, width), bases[:, 1].reshape(2 * rank, width)], axis=1
        )
        both = jnp.concatenate([first, second], axis=1)
        return lax.dot_general(flat, both, LANES, preferred_element_type=F32)

    def part_copies(src, dst, sems, index, to_layer):
        copies = []
        slot = lax.rem(leaf, half)
        for other in range(half):
            copies.append(remote(
                src.at[0], dst.at[slot], sems, index + (other,),
                to_layer, (1 - upper) * half + other, index + (slot,),
            ))
        slot = half + lax.rem(leaf, quarter)
        sibling = lower + 1 - 2 * lax.rem(lower, 2)
        for other in range(quarter):
            copies.append(remote(
                src.at[1], dst.at[slot], sems, index + (half + other,),
                to_layer, sibling * quarter + other, index + (slot,),
            ))
        return copies

    def part_arrivals(src, dst, sems, index):
        for slot in range(half + quarter):
            pltpu.make_async_copy(
                dst.at[slot], dst.at[slot], sems.at[(1,) + index + (slot,)]
            ).wait()

    def near_leaf(q, field, low, high):
        pieces = []
        for at in (q, q - 1, q + 1):
            if at < 0:
                view = low
            elif at >= count:
                view = high
            else:
                view = field.at[:, :, pl.ds(at * cells, cells)]
            pieces.append(stacked(view[0], view[1]))
        lhs = jnp.concatenate([a for a, _ in pieces] + [b for _, b in pieces], axis=1)
        rhs = jnp.concatenate(
            [near[q, s, 0] for s in range(3)] + [near[q, s, 1] for s in range(3)], axis=1
        )
        return lax.dot_general(lhs, rhs, LANES, preferred_element_type=F32)

    def coefficients(parts):
        first = parts[0].astype(F32)
        for slot in range(1, half):
            first = first + parts[slot].astype(F32)
        second = parts[half].astype(F32)
        for slot in range(1, quarter):
            second = second + parts[half + slot].astype(F32)
        turned = jnp.concatenate([first, second], axis=0).T
        size = turned.shape[0] // 2
        swapped = jnp.concatenate([-turned[size:], turned[:size]], axis=0)
        return turned.astype(BF16), swapped.astype(BF16)

    def far_leaf(q, coeff):
        span = pl.ds(q * cells, cells)
        return jnp.dot(coeff[0], left[0, :, span], preferred_element_type=F32) + jnp.dot(
            coeff[1], left[1, :, span], preferred_element_type=F32
        )

    loads[0].wait()
    loads[1].wait()
    first, second = stacked(source[0], source[1])
    sums = partial_sums(first, second, right[...])
    for level in range(2):
        part_sent[level] = sums[level * rank:(level + 1) * rank].astype(SUM_TYPE)

    pl.semaphore_wait(
        barrier,
        leafs - 1 + leafs * has_prev.astype(jnp.int32) + leafs * has_next.astype(jnp.int32),
    )

    to_high = remote(
        source.at[:, :, pl.ds(width - cells, cells)], rim.at[0], rim_sem, (0,), layer, leaf + 1
    )
    to_low = remote(source.at[:, :, pl.ds(0, cells)], rim.at[1], rim_sem, (1,), layer, leaf - 1)
    source_parts = part_copies(part_sent, part, part_sem, (), layer)
    down = remote(right, right_next, right_sem, (), layer - 1, leaf)
    pl.when(has_high)(to_high.start)
    pl.when(has_low)(to_low.start)
    for copy in source_parts:
        copy.start()
    pl.when(has_prev)(down.start)

    loads[2].wait()
    row_ids = lax.broadcasted_iota(jnp.int32, (rank, width), 0)
    for level, slot in ((0, upper), (1, 2 + lower)):
        keep = (row_ids < ranks_ref[0, slot]).astype(F32)
        for c in range(2):
            left[c, pl.ds(level * rank, rank), :] = (
                left_raw[level, c].astype(F32) * keep
            ).astype(BF16)

    for q in order:
        if q == order[max(count - 2, 0)]:
            pl.when(has_low)(to_high.wait_recv)
            pl.when(has_high)(to_low.wait_recv)
        near_loads[q].wait()
        inner[:, :, pl.ds(q * cells, cells)] = near_leaf(
            q, source, rim.at[0], rim.at[1]
        ).reshape(2, rows, cells)
    part_arrivals(part_sent, part, part_sem, ())
    coeff = coefficients(part)
    for q in range(count):
        span = pl.ds(q * cells, cells)
        inner[:, :, span] += far_leaf(q, coeff).reshape(2, rows, cells)

    in_flight = []
    for b in range(batches):
        span_rows = pl.ds(b * group, group)
        spans = [(0, width)]
        ahead = [
            remote(
                sent.at[b, :, :, pl.ds(*span)], moved.at[b, :, :, pl.ds(*span)],
                move_sem, (b, piece), layer + 1, leaf,
            )
            for piece, span in enumerate(spans)
        ]
        across_high = remote(
            moved.at[b, :, :, pl.ds(width - cells, cells)], moved_rim.at[b, 0],
            move_rim_sem, (b, 0), layer, leaf + 1,
        )
        across_low = remote(
            moved.at[b, :, :, pl.ds(0, cells)], moved_rim.at[b, 1],
            move_rim_sem, (b, 1), layer, leaf - 1,
        )
        ahead_high = remote(
            sent.at[b, :, :, pl.ds(width - cells, cells)], moved_rim.at[b, 0],
            move_rim_sem, (b, 0), layer + 1, leaf + 1,
        )
        ahead_low = remote(
            sent.at[b, :, :, pl.ds(0, cells)], moved_rim.at[b, 1],
            move_rim_sem, (b, 1), layer + 1, leaf - 1,
        )
        ahead_parts = part_copies(
            moved_part_sent.at[b], moved_part.at[b], move_part_sem, (b,), layer + 1
        )

        in_flight.append(
            (ahead, ahead_parts, across_low, across_high, ahead_high, ahead_low)
        )

        @pl.when(jnp.logical_not(has_prev))
        def _():
            out_ref[0, :, span_rows, :] = inner[:, span_rows, :].astype(BF16)

        @pl.when(has_prev)
        def _():
            ahead[0].wait_recv()
            pl.when(odd)(across_low.start)
            pl.when(even)(across_high.start)
            found = {}
            for q in order:
                if q == order[max(count - 2, 0)]:
                    pl.when(has_low)(ahead_high.wait_recv)
                    pl.when(has_high)(ahead_low.wait_recv)
                found[q] = near_leaf(q, moved.at[b], moved_rim.at[b, 0], moved_rim.at[b, 1])
            part_arrivals(moved_part_sent.at[b], moved_part.at[b], move_part_sem, (b,))
            coeff = coefficients(moved_part[b])
            for q in range(count):
                span = pl.ds(q * cells, cells)
                update = (found[q] + far_leaf(q, coeff)).reshape(2, group, cells)
                out_ref[0, :, span_rows, span] = (
                    inner[:, span_rows, span] - update
                ).astype(BF16)

        @pl.when(has_next)
        def _():
            swept = out_ref[0, :, span_rows, :].astype(F32)
            coupled = (coupling_ref[...].astype(F32)[None] * swept).astype(BF16)
            sent[b] = coupled
            ahead[0].start()
            first, second = stacked(coupled[0], coupled[1])
            if b == 0:
                down.wait_recv()
            sums = partial_sums(first, second, right_next[...])
            for level in range(2):
                moved_part_sent[b, level] = sums[level * rank:(level + 1) * rank].astype(SUM_TYPE)
            for copy in ahead_parts:
                copy.start()
            pl.when(odd & has_high)(ahead_high.start)
            pl.when(even & has_low)(ahead_low.start)

    pl.when(has_high)(to_high.wait_send)
    pl.when(has_low)(to_low.wait_send)
    for copy in source_parts:
        copy.wait_send()
    pl.when(has_prev)(down.wait_send)

    for b in range(batches):
        flights = in_flight[b]

        @pl.when(has_prev)
        def _():
            pl.when(odd)(flights[2].wait_send)
            pl.when(even)(flights[3].wait_send)

        @pl.when(has_next)
        def _():
            for copy in flights[0] + flights[1]:
                copy.wait_send()
            pl.when(odd & has_high)(flights[4].wait_send)
            pl.when(even & has_low)(flights[5].wait_send)


def body(layers, leafs, right_side, near_blocks, right_bases, left_bases, coupling, ranks):
    rows, width = right_side.shape[2:]
    cells = near_blocks.shape[-1]
    rank = right_bases.shape[3]
    count = width // cells
    batches = BATCHES
    group = rows // batches
    sources = leafs // 2 + leafs // 4
    anywhere = pl.BlockSpec(memory_space=pl.ANY)
    dma = pltpu.SemaphoreType.DMA
    return pl.pallas_call(
        functools.partial(kernel, layers, leafs, batches),
        out_shape=jax.ShapeDtypeStruct(right_side.shape, BF16),
        in_specs=[anywhere] * 4
        + [pl.BlockSpec(memory_space=pltpu.VMEM), pl.BlockSpec(memory_space=pltpu.SMEM)],
        out_specs=pl.BlockSpec(memory_space=pltpu.VMEM),
        scratch_shapes=[
            pltpu.VMEM((2, rows, width), BF16),
            pltpu.VMEM((count, 3, 2, cells, cells), BF16),
            pltpu.VMEM((2, 2, rank, width), BF16),
            pltpu.VMEM((2, 2, rank, width), BF16),
            pltpu.VMEM((2, 2, rank, width), BF16),
            pltpu.VMEM((2, 2 * rank, width), BF16),
            pltpu.VMEM((2, rows, width), F32),
            pltpu.VMEM((2, 2, rows, cells), BF16),
            pltpu.VMEM((sources, rank, 2 * rows), SUM_TYPE),
            pltpu.VMEM((2, rank, 2 * rows), SUM_TYPE),
            pltpu.VMEM((batches, 2, group, width), BF16),
            pltpu.VMEM((batches, 2, group, width), BF16),
            pltpu.VMEM((batches, 2, 2, group, cells), BF16),
            pltpu.VMEM((batches, sources, rank, 2 * group), SUM_TYPE),
            pltpu.VMEM((batches, 2, rank, 2 * group), SUM_TYPE),
            dma((3,)),
            dma((count,)),
            dma((2, 2)),
            dma((2, sources)),
            dma((2,)),
            dma((2, batches, 1)),
            dma((2, batches, 2)),
            dma((2, batches, sources)),
        ],
        compiler_params=pltpu.CompilerParams(collective_id=0, has_side_effects=True),
    )(right_side, near_blocks, right_bases, left_bases, coupling, ranks)


def solution(mesh):
    placed = (
        P("layer", None, None, "leaf"),
        P("layer", None, None, "leaf", None),
        P("layer", None, None, None, "leaf"),
        P("layer", None, None, None, "leaf"),
        P("layer", "leaf"),
        P("layer", None),
    )
    return jax.shard_map(
        functools.partial(body, mesh.shape["layer"], mesh.shape["leaf"]),
        mesh=mesh, in_specs=placed, out_specs=P("layer", None, None, "leaf"), check_vma=False,
    )
```

profile of v0, /device:TPU:25, one launch (start us, length us, event | category | flops | bytes accessed | tf_op | source)
XLA Modules:
  0.0 30.6 jit_solution(16732678619176337783)
XLA Ops:
  0.0 29.0 %shard_map.64 = bf16[1,2,32,1024]{3,2,1,0:T(8,128)(2,1)} custom-call(bf16[1,2,32,1024]{3,2,1,0:T(8,128)(2,1)} %source_hbm.1, bf16[1,3,2,1024,256]{4,3,2,1,0:T(8,128)(2,1)} %near_hbm.1, bf16[1,2,2,16,1024]{4,3,2,1,0:T(8,128)(2,1)} %right_hbm.1, bf16[1,2,2,16,1024]{4,3,2,1,0:T(8,128)(2,1)} %left_hbm.1, bf16[1,1024]{1,0:T(2,128)(2,1)} %coupling_ref.1, ...), custom_call_target="tpu_custom_call" | custom-call | tf_op jit(solution)/shard_map/pallas_call | solution.py:317
  29.0 1.6 %copy.8 = bf16[1,2,32,1024]{3,2,1,0:T(8,128)(2,1)} copy(bf16[1,2,32,1024]{3,2,1,0:T(8,128)(2,1)} %shard_map.64) | data formatting | bytes 262144
where the time goes:
time: 30.8 us; the launch traced here: 30.6 us
  Pallas kernels  29 us (94%)
  local copies, waits for them, and re-layouts  1.57 us (5%)
    pallas_call x1, Pallas kernels, body(): pl.pallas_call(functools.partial(kernel, layers, leafs, batches), out_sha...  29 us
    unnamed x1, local copies, waits for them, and re-layouts  1.57 us

commit v1 on v0

--- a/solution.py
+++ b/solution.py
@@ -16,9 +16,9 @@
 
 def kernel(
     layers, leafs, batches,
-    source_hbm, near_hbm, right_hbm, left_hbm, coupling_ref, ranks_ref,
+    source_hbm, near_hbm, right_hbm, left_hbm, coupling_hbm, ranks_hbm,
     out_ref,
-    source, near, right, right_next, left_raw, left, inner,
+    source, near, near_turned, right, right_next, left_raw, left, coupling_ref, ranks_ref, inner, found,
     rim, part, part_sent, moved, sent, moved_rim, moved_part, moved_part_sent,
     load_sem, near_sem, rim_sem, part_sem, right_sem, move_sem, move_rim_sem, move_part_sem,
 ):
@@ -47,6 +47,8 @@
         pltpu.make_async_copy(source_hbm.at[0], source, load_sem.at[0]),
         pltpu.make_async_copy(right_hbm.at[0], right, load_sem.at[1]),
         pltpu.make_async_copy(left_hbm.at[0], left_raw, load_sem.at[2]),
+        pltpu.make_async_copy(coupling_hbm, coupling_ref, load_sem.at[3]),
+        pltpu.make_async_copy(ranks_hbm, ranks_ref, load_sem.at[4]),
     ]
     near_loads = [
         pltpu.make_async_copy(
@@ -55,30 +57,30 @@
         for q in range(count)
     ]
     order = list(range(1, count - 1)) + ([0, count - 1] if count > 1 else [0])
+    barrier = pltpu.get_barrier_semaphore()
+
+    def greet(to_layer, to_leaf):
+        pl.semaphore_signal(
+            barrier, inc=1, device_id=(to_layer, to_leaf), device_id_type=pl.DeviceIdType.MESH
+        )
+
+    for step in range(1, leafs):
+        greet(layer, lax.rem(leaf + step, leafs))
+
+    @pl.when(has_prev)
+    def _():
+        for other in range(leafs):
+            greet(layer - 1, other)
+
+    @pl.when(has_next)
+    def _():
+        for other in range(leafs):
+            greet(layer + 1, other)
+
     for copy in loads:
         copy.start()
     for q in order:
         near_loads[q].start()
-
-    barrier = pltpu.get_barrier_semaphore()
-
-    def greet(to_layer, to_leaf):
-        pl.semaphore_signal(
-            barrier, inc=1, device_id=(to_layer, to_leaf), device_id_type=pl.DeviceIdType.MESH
-        )
-
-    for step in range(1, leafs):
-        greet(layer, lax.rem(leaf + step, leafs))
-
-    @pl.when(has_prev)
-    def _():
-        for other in range(leafs):
-            greet(layer - 1, other)
-
-    @pl.when(has_next)
-    def _():
-        for other in range(leafs):
-            greet(layer + 1, other)
 
     @pl.when(jnp.logical_not(has_low))
     def _():
@@ -125,7 +127,7 @@
                 dst.at[slot], dst.at[slot], sems.at[(1,) + index + (slot,)]
             ).wait()
 
-    def near_leaf(q, field, low, high):
+    def near_leaf(q, field, low, high, turned=False):
         pieces = []
         for at in (q, q - 1, q + 1):
             if at < 0:
@@ -136,6 +138,8 @@
                 view = field.at[:, :, pl.ds(at * cells, cells)]
             pieces.append(stacked(view[0], view[1]))
         lhs = jnp.concatenate([a for a, _ in pieces] + [b for _, b in pieces], axis=1)
+        if turned:
+            return jnp.dot(lhs, near_turned[q], preferred_element_type=F32)
         rhs = jnp.concatenate(
             [near[q, s, 0] for s in range(3)] + [near[q, s, 1] for s in range(3)], axis=1
         )
@@ -151,13 +155,11 @@
         turned = jnp.concatenate([first, second], axis=0).T
         size = turned.shape[0] // 2
         swapped = jnp.concatenate([-turned[size:], turned[:size]], axis=0)
-        return turned.astype(BF16), swapped.astype(BF16)
+        return jnp.concatenate([turned, swapped], axis=1).astype(BF16)
 
     def far_leaf(q, coeff):
         span = pl.ds(q * cells, cells)
-        return jnp.dot(coeff[0], left[0, :, span], preferred_element_type=F32) + jnp.dot(
-            coeff[1], left[1, :, span], preferred_element_type=F32
-        )
+        return jnp.dot(coeff, left[:, span], preferred_element_type=F32)
 
     loads[0].wait()
     loads[1].wait()
@@ -184,11 +186,13 @@
     pl.when(has_prev)(down.start)
 
     loads[2].wait()
+    loads[3].wait()
+    loads[4].wait()
     row_ids = lax.broadcasted_iota(jnp.int32, (rank, width), 0)
     for level, slot in ((0, upper), (1, 2 + lower)):
         keep = (row_ids < ranks_ref[0, slot]).astype(F32)
         for c in range(2):
-            left[c, pl.ds(level * rank, rank), :] = (
+            left[pl.ds((2 * c + level) * rank, rank), :] = (
                 left_raw[level, c].astype(F32) * keep
             ).astype(BF16)
 
@@ -205,6 +209,13 @@
     for q in range(count):
         span = pl.ds(q * cells, cells)
         inner[:, :, span] += far_leaf(q, coeff).reshape(2, rows, cells)
+
+    @pl.when(has_prev)
+    def _():
+        for q in range(count):
+            for c in range(2):
+                for s in range(3):
+                    near_turned[q, pl.ds((3 * c + s) * cells, cells), :] = near[q, s, c].T
 
     in_flight = []
     for b in range(batches):
@@ -250,12 +261,11 @@
             ahead[0].wait_recv()
             pl.when(odd)(across_low.start)
             pl.when(even)(across_high.start)
-            found = {}
             for q in order:
                 if q == order[max(count - 2, 0)]:
                     pl.when(has_low)(ahead_high.wait_recv)
                     pl.when(has_high)(ahead_low.wait_recv)
-                found[q] = near_leaf(q, moved.at[b], moved_rim.at[b, 0], moved_rim.at[b, 1])
+                found[q] = near_leaf(q, moved.at[b], moved_rim.at[b, 0], moved_rim.at[b, 1], True)
             part_arrivals(moved_part_sent.at[b], moved_part.at[b], move_part_sem, (b,))
             coeff = coefficients(moved_part[b])
             for q in range(count):
@@ -313,21 +323,25 @@
     group = rows // batches
     sources = leafs // 2 + leafs // 4
     anywhere = pl.BlockSpec(memory_space=pl.ANY)
+    vmem = pl.BlockSpec(memory_space=pltpu.VMEM)
     dma = pltpu.SemaphoreType.DMA
     return pl.pallas_call(
         functools.partial(kernel, layers, leafs, batches),
-        out_shape=jax.ShapeDtypeStruct(right_side.shape, BF16),
-        in_specs=[anywhere] * 4
-        + [pl.BlockSpec(memory_space=pltpu.VMEM), pl.BlockSpec(memory_space=pltpu.SMEM)],
-        out_specs=pl.BlockSpec(memory_space=pltpu.VMEM),
+        out_shape=pltpu.VMEM(right_side.shape, BF16),
+        in_specs=[anywhere] * 6,
+        out_specs=vmem,
         scratch_shapes=[
             pltpu.VMEM((2, rows, width), BF16),
             pltpu.VMEM((count, 3, 2, cells, cells), BF16),
+            pltpu.VMEM((count, 6 * cells, cells), BF16),
             pltpu.VMEM((2, 2, rank, width), BF16),
             pltpu.VMEM((2, 2, rank, width), BF16),
             pltpu.VMEM((2, 2, rank, width), BF16),
-            pltpu.VMEM((2, 2 * rank, width), BF16),
+            pltpu.VMEM((4 * rank, width), BF16),
+            pltpu.VMEM(coupling.shape, BF16),
+            pltpu.SMEM(ranks.shape, jnp.int32),
             pltpu.VMEM((2, rows, width), F32),
+            pltpu.VMEM((count, 2 * group, cells), F32),
             pltpu.VMEM((2, 2, rows, cells), BF16),
             pltpu.VMEM((sources, rank, 2 * rows), SUM_TYPE),
             pltpu.VMEM((2, rank, 2 * rows), SUM_TYPE),
@@ -336,7 +350,7 @@
             pltpu.VMEM((batches, 2, 2, group, cells), BF16),
             pltpu.VMEM((batches, sources, rank, 2 * group), SUM_TYPE),
             pltpu.VMEM((batches, 2, rank, 2 * group), SUM_TYPE),
-            dma((3,)),
+            dma((5,)),
             dma((count,)),
             dma((2, 2)),
             dma((2, sources)),

time: 30.8 us -> 26.1 us (0.85)
  Pallas kernels: 29 us -> 25.3 us
  local copies, waits for them, and re-layouts: 1.57 us -> 0.66 us
    pallas_call x1, Pallas kernels: 29 us -> 25.3 us  [body(): pl.pallas_call(functools.partial(kernel, layers, leafs, batches), out_sha...]
    unnamed x1, local copies, waits for them, and re-layouts: 1.57 us -> 0.66 us
where the time goes in v1:
time: 26.1 us; the launch traced here: 25.9 us
  Pallas kernels  25.3 us (97%)
  local copies, waits for them, and re-layouts  0.66 us (3%)
    pallas_call x1, Pallas kernels, body(): pl.pallas_call(functools.partial(kernel, layers, leafs, batches), out_sha...  25.3 us
    unnamed x1, local copies, waits for them, and re-layouts  0.66 us

profile of v1, /device:TPU:25, one launch (start us, length us, event | category | flops | bytes accessed | tf_op | source)
XLA Modules:
  0.0 25.9 jit_solution(9497293152041625881)
XLA Ops:
  0.0 25.3 %shard_map.64 = bf16[1,2,32,1024]{3,2,1,0:T(8,128)(2,1)S(1)} custom-call(bf16[1,2,32,1024]{3,2,1,0:T(8,128)(2,1)} %source_hbm.1, bf16[1,3,2,1024,256]{4,3,2,1,0:T(8,128)(2,1)} %near_hbm.1, bf16[1,2,2,16,1024]{4,3,2,1,0:T(8,128)(2,1)} %right_hbm.1, bf16[1,2,2,16,1024]{4,3,2,1,0:T(8,128)(2,1)} %left_hbm.1, bf16[1,1024]{1,0:T(2,128)(2,1)} %coupling_hbm.1, ...), custom_call_target="tpu_custom_call" | custom-call | tf_op jit(solution)/shard_map/pallas_call | solution.py:328
  25.3 0.7 %copy.8 = bf16[1,2,32,1024]{3,2,1,0:T(8,128)(2,1)} copy(bf16[1,2,32,1024]{3,2,1,0:T(8,128)(2,1)S(1)} %shard_map.64) | data formatting | bytes 262144

commit v2 on v1

v2 whole, which is shorter than its diff:
```python
import functools

import jax
import jax.numpy as jnp
from jax import lax
from jax.experimental import pallas as pl
from jax.experimental.pallas import tpu as pltpu
from jax.sharding import PartitionSpec as P

BATCHES = 2
FOLD = 8
F32 = jnp.float32
BF16 = jnp.bfloat16
LANES = (((1,), (1,)), ((), ()))


def kernel(
    layers, leafs, batches,
    source_hbm, near_hbm, right_hbm, left_hbm, coupling_hbm, ranks_hbm,
    out_ref,
    source, near, near_turned, right, right_next, left_raw, left, coupling_ref, ranks_ref,
    inner, base, rim, part, part_sent, moved, sent, moved_rim, moved_part, moved_part_sent,
    load_sem, near_sem, rim_sem, part_sem, right_sem, move_sem, move_rim_sem, move_part_sem, sent_sem,
):
    layer = lax.axis_index("layer")
    leaf = lax.axis_index("leaf")
    rows, width = source.shape[1], source.shape[2]
    cells = near.shape[-1]
    count = width // cells
    rank = right.shape[2]
    group = rows // batches
    half, quarter = leafs // 2, leafs // 4
    upper, lower = leaf // half, leaf // quarter
    has_low, has_high = leaf > 0, leaf < leafs - 1
    has_prev, has_next = layer > 0, layer < layers - 1
    edges = [0, count - 1] if count > 1 else [0]

    def remote(src, dst, sems, index, to_layer, to_leaf):
        return pltpu.make_async_remote_copy(
            src_ref=src, dst_ref=dst,
            send_sem=sems.at[(0,) + index],
            recv_sem=sems.at[(1,) + index],
            device_id=(to_layer, to_leaf), device_id_type=pl.DeviceIdType.MESH,
        )

    barrier = pltpu.get_barrier_semaphore()

    def greet(to_layer, to_leaf):
        pl.semaphore_signal(
            barrier, inc=1, device_id=(to_layer, to_leaf), device_id_type=pl.DeviceIdType.MESH
        )

    for step in range(1, leafs):
        greet(layer, lax.rem(leaf + step, leafs))

    @pl.when(has_prev)
    def _():
        for other in range(leafs):
            greet(layer - 1, other)

    @pl.when(has_next)
    def _():
        for other in range(leafs):
            greet(layer + 1, other)

    loads = [
        pltpu.make_async_copy(source_hbm.at[0], source, load_sem.at[0]),
        pltpu.make_async_copy(right_hbm.at[0], right, load_sem.at[1]),
        pltpu.make_async_copy(left_hbm.at[0], left_raw, load_sem.at[2]),
        pltpu.make_async_copy(coupling_hbm, coupling_ref, load_sem.at[3]),
        pltpu.make_async_copy(ranks_hbm, ranks_ref, load_sem.at[4]),
    ]
    near_loads = [
        pltpu.make_async_copy(
            near_hbm.at[0, :, :, pl.ds(q * cells, cells), :], near.at[q], near_sem.at[q]
        )
        for q in range(count)
    ]
    for copy in loads + near_loads:
        copy.start()

    @pl.when(jnp.logical_not(has_low))
    def _():
        rim[0] = jnp.zeros(rim.shape[1:], BF16)
        for b in range(batches):
            moved_rim[b, 0] = jnp.zeros(moved_rim.shape[2:], BF16)

    @pl.when(jnp.logical_not(has_high))
    def _():
        rim[1] = jnp.zeros(rim.shape[1:], BF16)
        for b in range(batches):
            moved_rim[b, 1] = jnp.zeros(moved_rim.shape[2:], BF16)

    def block(q):
        return pl.ds(q * cells, cells)

    def stacked(real, imag):
        return jnp.concatenate(
            [
                jnp.concatenate([real, imag], axis=0),
                jnp.concatenate([-imag, real], axis=0),
            ],
            axis=1,
        )

    def piece(field, q):
        return stacked(field[0, :, block(q)], field[1, :, block(q)])

    def sides(q):
        return [0] + ([1] if q > 0 else []) + ([2] if q < count - 1 else [])

    def shifted(q, s):
        return q + (0, -1, 1)[s]

    def folded(pieces, bases):
        total = None
        for q in range(count):
            flat = jnp.concatenate(
                [bases[:, c, :, block(q)].reshape(2 * rank, cells) for c in range(2)], axis=1
            )
            term = lax.dot_general(pieces[q], flat, LANES, preferred_element_type=F32)
            total = term if total is None else total + term
        return jnp.concatenate(
            [total[at:at + FOLD] for at in range(0, total.shape[0], FOLD)], axis=1
        ).astype(BF16)

    def part_copies(src, dst, sems, index, to_layer):
        copies = []
        slot = lax.rem(leaf, half)
        for other in range(half):
            copies.append(remote(
                src, dst.at[slot], sems, index,
                to_layer, (1 - upper) * half + other,
            ))
        slot = half + lax.rem(leaf, quarter)
        sibling = lower + 1 - 2 * lax.rem(lower, 2)
        for other in range(quarter):
            copies.append(remote(
                src, dst.at[slot], sems, index,
                to_layer, sibling * quarter + other,
            ))
        return copies

    def part_waits(dst, sems, index, way):
        pltpu.make_async_copy(dst, dst, sems.at[(way,) + index]).wait()

    def coefficients(parts):
        first = parts[0].astype(F32)
        for slot in range(1, half):
            first = first + parts[slot].astype(F32)
        second = parts[half].astype(F32)
        for slot in range(1, quarter):
            second = second + parts[half + slot].astype(F32)
        column = lax.broadcasted_iota(jnp.int32, first.shape, 1)
        both = jnp.where(lax.rem(column, 2 * rank) < rank, first, second)
        turned = jnp.concatenate(
            [both[:, at:at + 2 * rank] for at in range(0, both.shape[1], 2 * rank)], axis=0
        )
        size = turned.shape[0] // 2
        swapped = jnp.concatenate([-turned[size:], turned[:size]], axis=0)
        return jnp.concatenate([turned, swapped], axis=1).astype(BF16)

    def far_leaf(q, coeff):
        return jnp.dot(coeff, left[:, block(q)], preferred_element_type=F32)

    def plain_dot(q, s, value):
        rhs = jnp.concatenate([near[q, s, 0], near[q, s, 1]], axis=1)
        return lax.dot_general(value, rhs, LANES, preferred_element_type=F32)

    def turned_dot(q, chosen, values):
        rhs = [near_turned[q, pl.ds(s * 2 * cells, 2 * cells), :] for s in chosen]
        return jnp.dot(
            jnp.concatenate(values, axis=1), jnp.concatenate(rhs, axis=0),
            preferred_element_type=F32,
        )

    loads[0].wait()
    loads[1].wait()
    source_pieces = [piece(source, q) for q in range(count)]
    part_sent[...] = folded(source_pieces, right)

    pl.semaphore_wait(
        barrier,
        leafs - 1 + leafs * has_prev.astype(jnp.int32) + leafs * has_next.astype(jnp.int32),
    )

    to_high = remote(
        source.at[:, :, block(count - 1)], rim.at[0], rim_sem, (0,), layer, leaf + 1
    )
    to_low = remote(source.at[:, :, block(0)], rim.at[1], rim_sem, (1,), layer, leaf - 1)
    source_parts = part_copies(part_sent, part, part_sem, (), layer)
    down = remote(right, right_next, right_sem, (), layer - 1, leaf)
    for copy in source_parts:
        copy.start()
    pl.when(has_high)(to_high.start)
    pl.when(has_low)(to_low.start)
    pl.when(has_prev)(down.start)

    loads[2].wait()
    loads[3].wait()
    loads[4].wait()
    row_ids = lax.broadcasted_iota(jnp.int32, (rank, width), 0)
    for level, slot in ((0, upper), (1, 2 + lower)):
        keep = (row_ids < ranks_ref[0, slot]).astype(F32)
        for c in range(2):
            left[pl.ds((2 * c + level) * rank, rank), :] = (
                left_raw[level, c].astype(F32) * keep
            ).astype(BF16)

    for q in range(count):
        near_loads[q].wait()
        value = None
        for s in sides(q):
            term = plain_dot(q, s, source_pieces[shifted(q, s)])
            value = term if value is None else value + term
        inner[:, :, block(q)] = value.reshape(2, rows, cells)
    pl.when(has_low)(to_high.wait_recv)
    pl.when(has_high)(to_low.wait_recv)
    for q, s, side in ((0, 1, 0), (count - 1, 2, 1)):
        inner[:, :, block(q)] += plain_dot(q, s, stacked(rim[side, 0], rim[side, 1])).reshape(
            2, rows, cells
        )
    part_waits(part, part_sem, (), 1)
    coeff = coefficients(part)
    for q in range(count):
        inner[:, :, block(q)] += far_leaf(q, coeff).reshape(2, rows, cells)

    @pl.when(has_prev)
    def _():
        for q in range(count):
            for s in range(3):
                for c in range(2):
                    near_turned[q, pl.ds((2 * s + c) * cells, cells), :] = near[q, s, c].T

    def rows_of(b):
        return pl.ds(b * group, group)

    def ahead_main(b):
        pairs = [(block(q), 0) for q in edges]
        if count > 2:
            pairs.append((pl.ds(cells, width - 2 * cells), 1))
        return [
            pltpu.make_async_remote_copy(
                src_ref=sent.at[b, :, :, span], dst_ref=moved.at[b, :, :, span],
                send_sem=sent_sem.at[0], recv_sem=move_sem.at[b, kind],
                device_id=(layer + 1, leaf), device_id_type=pl.DeviceIdType.MESH,
            )
            for span, kind in pairs
        ]

    def rim_copy(source_ref, q, b, side, to_layer, to_leaf):
        return pltpu.make_async_remote_copy(
            src_ref=source_ref.at[b, :, :, block(q)], dst_ref=moved_rim.at[b, side],
            send_sem=sent_sem.at[1 + side], recv_sem=move_rim_sem.at[b, side],
            device_id=(to_layer, to_leaf), device_id_type=pl.DeviceIdType.MESH,
        )

    def ahead_high(b):
        return rim_copy(sent, count - 1, b, 0, layer + 1, leaf + 1)

    def ahead_low(b):
        return rim_copy(sent, 0, b, 1, layer + 1, leaf - 1)

    def ahead_parts(b):
        return part_copies(
            moved_part_sent.at[b], moved_part.at[b], move_part_sem, (b,), layer + 1
        )

    def receive(b):
        view = moved.at[b, :, :, pl.ds(0, len(edges) * cells)]
        pltpu.make_async_copy(view, view, move_sem.at[b, 0]).wait()
        if count > 2:
            view = moved.at[b, :, :, pl.ds(cells, width - 2 * cells)]
            pltpu.make_async_copy(view, view, move_sem.at[b, 1]).wait()
        pl.when(has_low)(ahead_high(b).wait_recv)
        pl.when(has_high)(ahead_low(b).wait_recv)
        pieces = [stacked(moved_rim[b, 0, 0], moved_rim[b, 0, 1])]
        pieces += [piece(moved.at[b], q) for q in range(count)]
        pieces += [stacked(moved_rim[b, 1, 0], moved_rim[b, 1, 1])]
        for q in range(count):
            base[q] = inner[:, rows_of(b), block(q)].reshape(2 * group, cells) - turned_dot(
                q, range(3), [pieces[q + 1], pieces[q], pieces[q + 2]]
            )
        part_waits(moved_part.at[b], move_part_sem, (b,), 1)
        coeff = coefficients(moved_part[b])
        fields = []
        for q in range(count):
            swept = (base[q] - far_leaf(q, coeff)).astype(BF16).reshape(2, group, cells)
            out_ref[0, :, rows_of(b), block(q)] = swept
            fields.append(swept)
        return fields

    def emit(b, fields, first):
        coupled = []
        for q in range(count):
            value = (coupling_ref[:, block(q)].astype(F32)[None] * fields[q].astype(F32)).astype(BF16)
            sent[b, :, :, block(q)] = value
            coupled.append(value)
        pl.when(has_high)(ahead_high(b).start)
        pl.when(has_low)(ahead_low(b).start)
        if first and b == 0:
            for copy in ahead_main(b):
                copy.start()
        if b == 0:
            down.wait_recv()
        moved_part_sent[b] = folded([stacked(v[0], v[1]) for v in coupled], right_next)
        for copy in ahead_parts(b):
            copy.start()
        if not (first and b == 0):
            for copy in ahead_main(b):
                copy.start()

    @pl.when(jnp.logical_not(has_prev))
    def _():
        for b in range(batches):
            out_ref[0, :, rows_of(b), :] = inner[:, rows_of(b), :].astype(BF16)

            @pl.when(has_next)
            def _():
                emit(b, [out_ref[0, :, rows_of(b), block(q)] for q in range(count)], True)

    @pl.when(has_prev & has_next)
    def _():
        for b in range(batches):
            emit(b, receive(b), False)

    @pl.when(has_prev & jnp.logical_not(has_next))
    def _():
        for b in range(batches):
            receive(b)

    pl.when(has_high)(to_high.wait_send)
    pl.when(has_low)(to_low.wait_send)
    part_waits(part, part_sem, (), 0)
    pl.when(has_prev)(down.wait_send)

    def drained(ref, index):
        pltpu.make_async_copy(ref, ref, sent_sem.at[index]).wait()

    @pl.when(has_next)
    def _():
        drained(sent, 0)
        pl.when(has_high)(lambda: drained(moved_rim.at[:, 0], 1))
        pl.when(has_low)(lambda: drained(moved_rim.at[:, 1], 2))
        for b in range(batches):
            part_waits(moved_part.at[b], move_part_sem, (b,), 0)


def body(layers, leafs, right_side, near_blocks, right_bases, left_bases, coupling, ranks):
    rows, width = right_side.shape[2:]
    cells = near_blocks.shape[-1]
    rank = right_bases.shape[3]
    count = width // cells
    batches = BATCHES
    group = rows // batches
    sources = leafs // 2 + leafs // 4
    dma = pltpu.SemaphoreType.DMA

    def fold_shape(size):
        return (FOLD, 2 * size // FOLD * 2 * rank)

    return pl.pallas_call(
        functools.partial(kernel, layers, leafs, batches),
        out_shape=pltpu.VMEM(right_side.shape, BF16),
        in_specs=[pl.BlockSpec(memory_space=pl.ANY)] * 6,
        out_specs=pl.BlockSpec(memory_space=pltpu.VMEM),
        scratch_shapes=[
            pltpu.VMEM((2, rows, width), BF16),
            pltpu.VMEM((count, 3, 2, cells, cells), BF16),
            pltpu.VMEM((count, 6 * cells, cells), BF16),
            pltpu.VMEM((2, 2, rank, width), BF16),
            pltpu.VMEM((2, 2, rank, width), BF16),
            pltpu.VMEM((2, 2, rank, width), BF16),
            pltpu.VMEM((4 * rank, width), BF16),
            pltpu.VMEM(coupling.shape, BF16),
            pltpu.SMEM(ranks.shape, jnp.int32),
            pltpu.VMEM((2, rows, width), F32),
            pltpu.VMEM((count, 2 * group, cells), F32),
            pltpu.VMEM((2, 2, rows, cells), BF16),
            pltpu.VMEM((sources,) + fold_shape(rows), BF16),
            pltpu.VMEM(fold_shape(rows), BF16),
            pltpu.VMEM((batches, 2, group, width), BF16),
            pltpu.VMEM((batches, 2, group, width), BF16),
            pltpu.VMEM((batches, 2, 2, group, cells), BF16),
            pltpu.VMEM((batches, sources) + fold_shape(group), BF16),
            pltpu.VMEM((batches,) + fold_shape(group), BF16),
            dma((5,)),
            dma((count,)),
            dma((2, 2)),
            dma((2,)),
            dma((2,)),
            dma((batches, 2)),
            dma((batches, 2)),
            dma((2, batches)),
            dma((3,)),
        ],
        compiler_params=pltpu.CompilerParams(collective_id=0, has_side_effects=True),
    )(right_side, near_blocks, right_bases, left_bases, coupling, ranks)


def solution(mesh):
    placed = (
        P("layer", None, None, "leaf"),
        P("layer", None, None, "leaf", None),
        P("layer", None, None, None, "leaf"),
        P("layer", None, None, None, "leaf"),
        P("layer", "leaf"),
        P("layer", None),
    )
    return jax.shard_map(
        functools.partial(body, mesh.shape["layer"], mesh.shape["leaf"]),
        mesh=mesh, in_specs=placed, out_specs=P("layer", None, None, "leaf"), check_vma=False,
    )
```

time: 26.1 us -> 24.8 us (0.950)
  Pallas kernels: 25.3 us -> 24 us
    pallas_call x1, Pallas kernels: 25.3 us -> 24 us  [body(): pl.pallas_call(functools.partial(kernel, layers, leafs, batches), out_sha...]
where the time goes in v2:
time: 24.8 us; the launch traced here: 24.6 us
  Pallas kernels  24 us (97%)
  local copies, waits for them, and re-layouts  0.66 us (3%)
    pallas_call x1, Pallas kernels, body(): pl.pallas_call(functools.partial(kernel, layers, leafs, batches), out_sha...  24 us
    unnamed x1, local copies, waits for them, and re-layouts  0.66 us

profile of v2, /device:TPU:25, one launch (start us, length us, event | category | flops | bytes accessed | tf_op | source)
XLA Modules:
  0.0 24.6 jit_solution(6777271283864981965)
XLA Ops:
  0.0 24.0 %shard_map.64 = bf16[1,2,32,1024]{3,2,1,0:T(8,128)(2,1)S(1)} custom-call(bf16[1,2,32,1024]{3,2,1,0:T(8,128)(2,1)} %source_hbm.1, bf16[1,3,2,1024,256]{4,3,2,1,0:T(8,128)(2,1)} %near_hbm.1, bf16[1,2,2,16,1024]{4,3,2,1,0:T(8,128)(2,1)} %right_hbm.1, bf16[1,2,2,16,1024]{4,3,2,1,0:T(8,128)(2,1)} %left_hbm.1, bf16[1,1024]{1,0:T(2,128)(2,1)} %coupling_hbm.1, ...), custom_call_target="tpu_custom_call" | custom-call | tf_op jit(solution)/shard_map/pallas_call | solution.py:362
  24.0 0.7 %copy.8 = bf16[1,2,32,1024]{3,2,1,0:T(8,128)(2,1)} copy(bf16[1,2,32,1024]{3,2,1,0:T(8,128)(2,1)S(1)} %shard_map.64) | data formatting | bytes 262144

commit v3 on v2

--- a/solution.py
+++ b/solution.py
@@ -7,8 +7,8 @@
 from jax.experimental.pallas import tpu as pltpu
 from jax.sharding import PartitionSpec as P
 
-BATCHES = 2
-FOLD = 8
+BATCHES = 4
+TILE = 128
 F32 = jnp.float32
 BF16 = jnp.bfloat16
 LANES = (((1,), (1,)), ((), ()))
@@ -20,7 +20,7 @@
     out_ref,
     source, near, near_turned, right, right_next, left_raw, left, coupling_ref, ranks_ref,
     inner, base, rim, part, part_sent, moved, sent, moved_rim, moved_part, moved_part_sent,
-    load_sem, near_sem, rim_sem, part_sem, right_sem, move_sem, move_rim_sem, move_part_sem, sent_sem,
+    load_sem, near_sem, rim_sem, part_sem, right_sem, move_sem, move_rim_sem, move_part_sem, sent_sem, ready_sem,
 ):
     layer = lax.axis_index("layer")
     leaf = lax.axis_index("leaf")
@@ -53,15 +53,8 @@
     for step in range(1, leafs):
         greet(layer, lax.rem(leaf + step, leafs))
 
-    @pl.when(has_prev)
-    def _():
-        for other in range(leafs):
-            greet(layer - 1, other)
-
-    @pl.when(has_next)
-    def _():
-        for other in range(leafs):
-            greet(layer + 1, other)
+    pl.when(has_prev)(lambda: greet(layer - 1, leaf))
+    pl.when(has_next)(lambda: greet(layer + 1, leaf))
 
     loads = [
         pltpu.make_async_copy(source_hbm.at[0], source, load_sem.at[0]),
@@ -120,8 +113,9 @@
             )
             term = lax.dot_general(pieces[q], flat, LANES, preferred_element_type=F32)
             total = term if total is None else total + term
+        height = max(total.shape[0] * total.shape[1] // TILE, 1)
         return jnp.concatenate(
-            [total[at:at + FOLD] for at in range(0, total.shape[0], FOLD)], axis=1
+            [total[at:at + height] for at in range(0, total.shape[0], height)], axis=1
         ).astype(BF16)
 
     def part_copies(src, dst, sems, index, to_layer):
@@ -180,8 +174,7 @@
     part_sent[...] = folded(source_pieces, right)
 
     pl.semaphore_wait(
-        barrier,
-        leafs - 1 + leafs * has_prev.astype(jnp.int32) + leafs * has_next.astype(jnp.int32),
+        barrier, leafs - 1 + has_prev.astype(jnp.int32) + has_next.astype(jnp.int32)
     )
 
     to_high = remote(
@@ -189,6 +182,13 @@
     )
     to_low = remote(source.at[:, :, block(0)], rim.at[1], rim_sem, (1,), layer, leaf - 1)
     source_parts = part_copies(part_sent, part, part_sem, (), layer)
+
+    @pl.when(has_prev)
+    def _():
+        pl.semaphore_signal(
+            ready_sem, inc=1, device_id=(layer - 1, leaf), device_id_type=pl.DeviceIdType.MESH
+        )
+
     down = remote(right, right_next, right_sem, (), layer - 1, leaf)
     for copy in source_parts:
         copy.start()
@@ -232,6 +232,8 @@
                 for c in range(2):
                     near_turned[q, pl.ds((2 * s + c) * cells, cells), :] = near[q, s, c].T
 
+    pl.when(has_next)(lambda: pl.semaphore_wait(ready_sem, 1))
+
     def rows_of(b):
         return pl.ds(b * group, group)
 
@@ -266,26 +268,73 @@
             moved_part_sent.at[b], moved_part.at[b], move_part_sem, (b,), layer + 1
         )
 
-    def receive(b):
+    def wait_edges(b):
         view = moved.at[b, :, :, pl.ds(0, len(edges) * cells)]
         pltpu.make_async_copy(view, view, move_sem.at[b, 0]).wait()
+
+    def wait_middle(b):
         if count > 2:
             view = moved.at[b, :, :, pl.ds(cells, width - 2 * cells)]
             pltpu.make_async_copy(view, view, move_sem.at[b, 1]).wait()
+
+    def wait_rims(b):
         pl.when(has_low)(ahead_high(b).wait_recv)
         pl.when(has_high)(ahead_low(b).wait_recv)
+
+    def receive_whole(b):
+        wait_edges(b)
+        wait_middle(b)
+        wait_rims(b)
+        part_waits(moved_part.at[b], move_part_sem, (b,), 1)
+        coeff = coefficients(moved_part[b])
         pieces = [stacked(moved_rim[b, 0, 0], moved_rim[b, 0, 1])]
         pieces += [piece(moved.at[b], q) for q in range(count)]
         pieces += [stacked(moved_rim[b, 1, 0], moved_rim[b, 1, 1])]
-        for q in range(count):
-            base[q] = inner[:, rows_of(b), block(q)].reshape(2 * group, cells) - turned_dot(
-                q, range(3), [pieces[q + 1], pieces[q], pieces[q + 2]]
+        fields = []
+        for q in range(count):
+            lhs = jnp.concatenate([pieces[q + 1], pieces[q], pieces[q + 2], coeff], axis=1)
+            rhs = jnp.concatenate([near_turned[q], left[:, block(q)]], axis=0)
+            value = inner[:, rows_of(b), block(q)].reshape(2 * group, cells) - jnp.dot(
+                lhs, rhs, preferred_element_type=F32
             )
+            swept = value.astype(BF16).reshape(2, group, cells)
+            out_ref[0, :, rows_of(b), block(q)] = swept
+            fields.append(swept)
+        return fields
+
+    def receive(b):
+        if b > 0:
+            return receive_whole(b)
+        def gathered(q, chosen):
+            return turned_dot(q, chosen, [pieces[shifted(q, s)] for s in chosen])
+
+        wait_edges(b)
+        pieces = {q: piece(moved.at[b], q) for q in edges}
+        left_over = {}
+        for q in range(count):
+            value = inner[:, rows_of(b), block(q)].reshape(2 * group, cells)
+            chosen = [s for s in sides(q) if shifted(q, s) in pieces]
+            left_over[q] = [s for s in sides(q) if s not in chosen]
+            base[q] = value - gathered(q, chosen) if chosen else value
+        wait_middle(b)
+        pieces.update({q: piece(moved.at[b], q) for q in range(1, count - 1)})
+        for q in range(count):
+            if left_over[q]:
+                base[q] -= gathered(q, left_over[q])
+        wait_rims(b)
         part_waits(moved_part.at[b], move_part_sem, (b,), 1)
         coeff = coefficients(moved_part[b])
         fields = []
         for q in range(count):
-            swept = (base[q] - far_leaf(q, coeff)).astype(BF16).reshape(2, group, cells)
+            values, weights = [coeff], [left[:, block(q)]]
+            for at, s, side in ((0, 1, 0), (count - 1, 2, 1)):
+                if at == q:
+                    values.append(stacked(moved_rim[b, side, 0], moved_rim[b, side, 1]))
+                    weights.append(near_turned[q, pl.ds(s * 2 * cells, 2 * cells), :])
+            value = base[q]
+            for one, weight in zip(values, weights):
+                value = value - jnp.dot(one, weight, preferred_element_type=F32)
+            swept = value.astype(BF16).reshape(2, group, cells)
             out_ref[0, :, rows_of(b), block(q)] = swept
             fields.append(swept)
         return fields
@@ -296,19 +345,22 @@
             value = (coupling_ref[:, block(q)].astype(F32)[None] * fields[q].astype(F32)).astype(BF16)
             sent[b, :, :, block(q)] = value
             coupled.append(value)
-        pl.when(has_high)(ahead_high(b).start)
-        pl.when(has_low)(ahead_low(b).start)
-        if first and b == 0:
+        def send_field():
+            pl.when(has_high)(ahead_high(b).start)
+            pl.when(has_low)(ahead_low(b).start)
             for copy in ahead_main(b):
                 copy.start()
+
+        early = first and b == 0
+        if early:
+            send_field()
         if b == 0:
             down.wait_recv()
         moved_part_sent[b] = folded([stacked(v[0], v[1]) for v in coupled], right_next)
         for copy in ahead_parts(b):
             copy.start()
-        if not (first and b == 0):
-            for copy in ahead_main(b):
-                copy.start()
+        if not early:
+            send_field()
 
     @pl.when(jnp.logical_not(has_prev))
     def _():
@@ -357,7 +409,8 @@
     dma = pltpu.SemaphoreType.DMA
 
     def fold_shape(size):
-        return (FOLD, 2 * size // FOLD * 2 * rank)
+        height = max(4 * size * rank // TILE, 1)
+        return (height, 4 * size * rank // height)
 
     return pl.pallas_call(
         functools.partial(kernel, layers, leafs, batches),
@@ -393,6 +446,7 @@
             dma((batches, 2)),
             dma((2, batches)),
             dma((3,)),
+            pltpu.SemaphoreType.REGULAR,
         ],
         compiler_params=pltpu.CompilerParams(collective_id=0, has_side_effects=True),
     )(right_side, near_blocks, right_bases, left_bases, coupling, ranks)

time: 24.8 us -> 23.4 us (0.944)
  Pallas kernels: 24 us -> 22.6 us
    pallas_call x1, Pallas kernels: 24 us -> 22.6 us  [body(): pl.pallas_call(functools.partial(kernel, layers, leafs, batches), out_sha...]
where the time goes in v3:
time: 23.4 us; the launch traced here: 23.2 us
  Pallas kernels  22.6 us (97%)
  local copies, waits for them, and re-layouts  0.66 us (3%)
    pallas_call x1, Pallas kernels, body(): pl.pallas_call(functools.partial(kernel, layers, leafs, batches), out_sha...  22.6 us
    unnamed x1, local copies, waits for them, and re-layouts  0.66 us

profile of v3, /device:TPU:25, one launch (start us, length us, event | category | flops | bytes accessed | tf_op | source)
XLA Modules:
  0.0 23.2 jit_solution(10888398564030454283)
XLA Ops:
  0.0 22.6 %shard_map.64 = bf16[1,2,32,1024]{3,2,1,0:T(8,128)(2,1)S(1)} custom-call(bf16[1,2,32,1024]{3,2,1,0:T(8,128)(2,1)} %source_hbm.1, bf16[1,3,2,1024,256]{4,3,2,1,0:T(8,128)(2,1)} %near_hbm.1, bf16[1,2,2,16,1024]{4,3,2,1,0:T(8,128)(2,1)} %right_hbm.1, bf16[1,2,2,16,1024]{4,3,2,1,0:T(8,128)(2,1)} %left_hbm.1, bf16[1,1024]{1,0:T(2,128)(2,1)} %coupling_hbm.1, ...), custom_call_target="tpu_custom_call" | custom-call | tf_op jit(solution)/shard_map/pallas_call | solution.py:415
  22.6 0.7 %copy.8 = bf16[1,2,32,1024]{3,2,1,0:T(8,128)(2,1)} copy(bf16[1,2,32,1024]{3,2,1,0:T(8,128)(2,1)S(1)} %shard_map.64) | data formatting | bytes 262144

commit v4 on v3

--- a/solution.py
+++ b/solution.py
@@ -19,8 +19,8 @@
     source_hbm, near_hbm, right_hbm, left_hbm, coupling_hbm, ranks_hbm,
     out_ref,
     source, near, near_turned, right, right_next, left_raw, left, coupling_ref, ranks_ref,
-    inner, base, rim, part, part_sent, moved, sent, moved_rim, moved_part, moved_part_sent,
-    load_sem, near_sem, rim_sem, part_sem, right_sem, move_sem, move_rim_sem, move_part_sem, sent_sem, ready_sem,
+    inner, base, rim, part, part_sent, moved, sent, moved_rim, moved_part, moved_part_sent, early_sent,
+    load_sem, rim_sem, part_sem, right_sem, move_sem, move_rim_sem, move_part_sem, sent_sem, ready_sem,
 ):
     layer = lax.axis_index("layer")
     leaf = lax.axis_index("leaf")
@@ -65,7 +65,7 @@
     ]
     near_loads = [
         pltpu.make_async_copy(
-            near_hbm.at[0, :, :, pl.ds(q * cells, cells), :], near.at[q], near_sem.at[q]
+            near_hbm.at[0, :, :, pl.ds(q * cells, cells), :], near.at[q], load_sem.at[5]
         )
         for q in range(count)
     ]
@@ -105,14 +105,24 @@
     def shifted(q, s):
         return q + (0, -1, 1)[s]
 
+    def level_sums(pieces, bases):
+        flat = [bases[c, :, block(q)] for q in range(count) for c in range(2)]
+        return lax.dot_general(
+            jnp.concatenate(pieces, axis=1), jnp.concatenate(flat, axis=1), LANES,
+            preferred_element_type=F32,
+        )
+
     def folded(pieces, bases):
-        total = None
-        for q in range(count):
-            flat = jnp.concatenate(
-                [bases[:, c, :, block(q)].reshape(2 * rank, cells) for c in range(2)], axis=1
-            )
-            term = lax.dot_general(pieces[q], flat, LANES, preferred_element_type=F32)
-            total = term if total is None else total + term
+        flat = [
+            bases[:, c, :, block(q)].reshape(2 * rank, cells) for q in range(count) for c in range(2)
+        ]
+        total = lax.dot_general(
+            jnp.concatenate(pieces, axis=1), jnp.concatenate(flat, axis=1), LANES,
+            preferred_element_type=F32,
+        )
+        return packed(total)
+
+    def packed(total):
         height = max(total.shape[0] * total.shape[1] // TILE, 1)
         return jnp.concatenate(
             [total[at:at + height] for at in range(0, total.shape[0], height)], axis=1
@@ -177,6 +187,16 @@
         barrier, leafs - 1 + has_prev.astype(jnp.int32) + has_next.astype(jnp.int32)
     )
 
+    downs = [
+        remote(right.at[level], right_next.at[level], right_sem, (level,), layer - 1, leaf)
+        for level in range(2)
+    ]
+
+    @pl.when(has_prev)
+    def _():
+        for copy in downs:
+            copy.start()
+
     to_high = remote(
         source.at[:, :, block(count - 1)], rim.at[0], rim_sem, (0,), layer, leaf + 1
     )
@@ -189,12 +209,10 @@
             ready_sem, inc=1, device_id=(layer - 1, leaf), device_id_type=pl.DeviceIdType.MESH
         )
 
-    down = remote(right, right_next, right_sem, (), layer - 1, leaf)
     for copy in source_parts:
         copy.start()
     pl.when(has_high)(to_high.start)
     pl.when(has_low)(to_low.start)
-    pl.when(has_prev)(down.start)
 
     loads[2].wait()
     loads[3].wait()
@@ -207,8 +225,8 @@
                 left_raw[level, c].astype(F32) * keep
             ).astype(BF16)
 
+    pltpu.make_async_copy(near, near, load_sem.at[5]).wait()
     for q in range(count):
-        near_loads[q].wait()
         value = None
         for s in sides(q):
             term = plain_dot(q, s, source_pieces[shifted(q, s)])
@@ -267,6 +285,11 @@
         return part_copies(
             moved_part_sent.at[b], moved_part.at[b], move_part_sem, (b,), layer + 1
         )
+
+    def early_parts():
+        return part_copies(
+            early_sent, moved_part.at[0], move_part_sem, (0,), layer + 1
+        )[:half]
 
     def wait_edges(b):
         view = moved.at[b, :, :, pl.ds(0, len(edges) * cells)]
@@ -302,8 +325,8 @@
             fields.append(swept)
         return fields
 
-    def receive(b):
-        if b > 0:
+    def receive(b, staged):
+        if not staged:
             return receive_whole(b)
         def gathered(q, chosen):
             return turned_dot(q, chosen, [pieces[shifted(q, s)] for s in chosen])
@@ -339,52 +362,87 @@
             fields.append(swept)
         return fields
 
-    def emit(b, fields, first):
+    def couple(b, fields):
         coupled = []
         for q in range(count):
             value = (coupling_ref[:, block(q)].astype(F32)[None] * fields[q].astype(F32)).astype(BF16)
             sent[b, :, :, block(q)] = value
-            coupled.append(value)
-        def send_field():
-            pl.when(has_high)(ahead_high(b).start)
-            pl.when(has_low)(ahead_low(b).start)
-            for copy in ahead_main(b):
-                copy.start()
-
-        early = first and b == 0
-        if early:
-            send_field()
-        if b == 0:
-            down.wait_recv()
-        moved_part_sent[b] = folded([stacked(v[0], v[1]) for v in coupled], right_next)
+            coupled.append(stacked(value[0], value[1]))
+        return coupled
+
+    def send_rims(b):
+        pl.when(has_high)(ahead_high(b).start)
+        pl.when(has_low)(ahead_low(b).start)
+
+    def send_main(b):
+        for copy in ahead_main(b):
+            copy.start()
+
+    def send_field(b):
+        send_rims(b)
+        send_main(b)
+
+    def send_parts(b, stacks):
+        moved_part_sent[b] = folded(stacks, right_next)
         for copy in ahead_parts(b):
             copy.start()
-        if not early:
-            send_field()
+
+    def emit_first():
+        for b in range(batches):
+            couple(b, [out_ref[0, :, rows_of(b), block(q)] for q in range(count)])
+            if b == 0:
+                send_field(b)
+        stacks = [piece(sent.at[0], q) for q in range(count)]
+        downs[0].wait_recv()
+        first_level = level_sums(stacks, right_next.at[0])
+        early_sent[...] = packed(
+            jnp.concatenate([first_level, jnp.zeros_like(first_level)], axis=1)
+        )
+        for copy in early_parts():
+            copy.start()
+        if batches > 1:
+            send_main(1)
+        downs[1].wait_recv()
+        second_level = level_sums(stacks, right_next.at[1])
+        moved_part_sent[0] = packed(jnp.concatenate([first_level, second_level], axis=1))
+        for copy in ahead_parts(0)[half:]:
+            copy.start()
+        if batches > 1:
+            send_rims(1)
+        for b in range(1, batches):
+            send_parts(b, [piece(sent.at[b], q) for q in range(count)])
+            if b > 1:
+                send_field(b)
 
     @pl.when(jnp.logical_not(has_prev))
     def _():
+        out_ref[0] = inner[...].astype(BF16)
+        pl.when(has_next)(emit_first)
+
+    @pl.when(has_prev & has_next)
+    def _():
         for b in range(batches):
-            out_ref[0, :, rows_of(b), :] = inner[:, rows_of(b), :].astype(BF16)
-
-            @pl.when(has_next)
-            def _():
-                emit(b, [out_ref[0, :, rows_of(b), block(q)] for q in range(count)], True)
-
-    @pl.when(has_prev & has_next)
+            if b == 0:
+                for copy in downs:
+                    copy.wait_recv()
+            stacks = couple(b, receive(b, b == 0))
+            send_parts(b, stacks)
+            send_field(b)
+
+    @pl.when(has_prev & jnp.logical_not(has_next))
     def _():
         for b in range(batches):
-            emit(b, receive(b), False)
-
-    @pl.when(has_prev & jnp.logical_not(has_next))
-    def _():
-        for b in range(batches):
-            receive(b)
+            receive(b, b == 0)
 
     pl.when(has_high)(to_high.wait_send)
     pl.when(has_low)(to_low.wait_send)
     part_waits(part, part_sem, (), 0)
-    pl.when(has_prev)(down.wait_send)
+
+    @pl.when(has_prev)
+    def _():
+        for copy in downs:
+            copy.wait_send()
+
 
     def drained(ref, index):
         pltpu.make_async_copy(ref, ref, sent_sem.at[index]).wait()
@@ -437,11 +495,11 @@
             pltpu.VMEM((batches, 2, 2, group, cells), BF16),
             pltpu.VMEM((batches, sources) + fold_shape(group), BF16),
             pltpu.VMEM((batches,) + fold_shape(group), BF16),
-            dma((5,)),
-            dma((count,)),
+            pltpu.VMEM(fold_shape(group), BF16),
+            dma((6,)),
             dma((2, 2)),
             dma((2,)),
-            dma((2,)),
+            dma((2, 2)),
             dma((batches, 2)),
             dma((batches, 2)),
             dma((2, batches)),

time: 23.4 us -> 23 us (0.983)
  Pallas kernels: 22.6 us -> 22.2 us
    pallas_call x1, Pallas kernels: 22.6 us -> 22.2 us  [body(): pl.pallas_call(functools.partial(kernel, layers, leafs, batches), out_sha...]
where the time goes in v4:
time: 23 us; the launch traced here: 22.9 us
  Pallas kernels  22.2 us (97%)
  local copies, waits for them, and re-layouts  0.66 us (3%)
    pallas_call x1, Pallas kernels, body(): pl.pallas_call(functools.partial(kernel, layers, leafs, batches), out_sha...  22.2 us
    unnamed x1, local copies, waits for them, and re-layouts  0.66 us

profile of v4, /device:TPU:25, one launch (start us, length us, event | category | flops | bytes accessed | tf_op | source)
XLA Modules:
  0.0 22.9 jit_solution(3013089186980262235)
XLA Ops:
  0.0 22.2 %shard_map.64 = bf16[1,2,32,1024]{3,2,1,0:T(8,128)(2,1)S(1)} custom-call(bf16[1,2,32,1024]{3,2,1,0:T(8,128)(2,1)} %source_hbm.1, bf16[1,3,2,1024,256]{4,3,2,1,0:T(8,128)(2,1)} %near_hbm.1, bf16[1,2,2,16,1024]{4,3,2,1,0:T(8,128)(2,1)} %right_hbm.1, bf16[1,2,2,16,1024]{4,3,2,1,0:T(8,128)(2,1)} %left_hbm.1, bf16[1,1024]{1,0:T(2,128)(2,1)} %coupling_hbm.1, ...), custom_call_target="tpu_custom_call" | custom-call | tf_op jit(solution)/shard_map/pallas_call | solution.py:473
  22.2 0.7 %copy.8 = bf16[1,2,32,1024]{3,2,1,0:T(8,128)(2,1)} copy(bf16[1,2,32,1024]{3,2,1,0:T(8,128)(2,1)S(1)} %shard_map.64) | data formatting | bytes 262144

commit v5 on v4

--- a/solution.py
+++ b/solution.py
@@ -19,7 +19,7 @@
     source_hbm, near_hbm, right_hbm, left_hbm, coupling_hbm, ranks_hbm,
     out_ref,
     source, near, near_turned, right, right_next, left_raw, left, coupling_ref, ranks_ref,
-    inner, base, rim, part, part_sent, moved, sent, moved_rim, moved_part, moved_part_sent, early_sent,
+    inner, base, rim, part, part_sent, moved, sent, moved_rim, moved_part, moved_part_sent,
     load_sem, rim_sem, part_sem, right_sem, move_sem, move_rim_sem, move_part_sem, sent_sem, ready_sem,
 ):
     layer = lax.axis_index("layer")
@@ -32,6 +32,7 @@
     half, quarter = leafs // 2, leafs // 4
     upper, lower = leaf // half, leaf // quarter
     has_low, has_high = leaf > 0, leaf < leafs - 1
+    odd, even = lax.rem(leaf, 2) == 1, lax.rem(leaf, 2) == 0
     has_prev, has_next = layer > 0, layer < layers - 1
     edges = [0, count - 1] if count > 1 else [0]
 
@@ -120,7 +121,7 @@
             jnp.concatenate(pieces, axis=1), jnp.concatenate(flat, axis=1), LANES,
             preferred_element_type=F32,
         )
-        return packed(total)
+        return [packed(total[:, level * rank:(level + 1) * rank]) for level in range(2)]
 
     def packed(total):
         height = max(total.shape[0] * total.shape[1] // TILE, 1)
@@ -133,14 +134,14 @@
         slot = lax.rem(leaf, half)
         for other in range(half):
             copies.append(remote(
-                src, dst.at[slot], sems, index,
+                src.at[0], dst.at[slot], sems, index,
                 to_layer, (1 - upper) * half + other,
             ))
         slot = half + lax.rem(leaf, quarter)
         sibling = lower + 1 - 2 * lax.rem(lower, 2)
         for other in range(quarter):
             copies.append(remote(
-                src, dst.at[slot], sems, index,
+                src.at[1], dst.at[slot], sems, index,
                 to_layer, sibling * quarter + other,
             ))
         return copies
@@ -155,11 +156,12 @@
         second = parts[half].astype(F32)
         for slot in range(1, quarter):
             second = second + parts[half + slot].astype(F32)
-        column = lax.broadcasted_iota(jnp.int32, first.shape, 1)
-        both = jnp.where(lax.rem(column, 2 * rank) < rank, first, second)
-        turned = jnp.concatenate(
-            [both[:, at:at + 2 * rank] for at in range(0, both.shape[1], 2 * rank)], axis=0
-        )
+        def unpacked(flat):
+            return jnp.concatenate(
+                [flat[:, at:at + rank] for at in range(0, flat.shape[1], rank)], axis=0
+            )
+
+        turned = jnp.concatenate([unpacked(first), unpacked(second)], axis=1)
         size = turned.shape[0] // 2
         swapped = jnp.concatenate([-turned[size:], turned[:size]], axis=0)
         return jnp.concatenate([turned, swapped], axis=1).astype(BF16)
@@ -181,7 +183,7 @@
     loads[0].wait()
     loads[1].wait()
     source_pieces = [piece(source, q) for q in range(count)]
-    part_sent[...] = folded(source_pieces, right)
+    part_sent[0], part_sent[1] = folded(source_pieces, right)
 
     pl.semaphore_wait(
         barrier, leafs - 1 + has_prev.astype(jnp.int32) + has_next.astype(jnp.int32)
@@ -281,15 +283,26 @@
     def ahead_low(b):
         return rim_copy(sent, 0, b, 1, layer + 1, leaf - 1)
 
+    def across_low(b):
+        return pltpu.make_async_remote_copy(
+            src_ref=moved.at[b, :, :, block(0)], dst_ref=moved_rim.at[b, 1],
+            send_sem=sent_sem.at[3], recv_sem=move_rim_sem.at[b, 1],
+            device_id=(layer, leaf - 1), device_id_type=pl.DeviceIdType.MESH,
+        )
+
+    def hand_across(b):
+        if b < batches:
+
+            @pl.when(odd)
+            def _():
+                wait_edges(b)
+                across_low(b).start()
+
     def ahead_parts(b):
         return part_copies(
             moved_part_sent.at[b], moved_part.at[b], move_part_sem, (b,), layer + 1
         )
 
-    def early_parts():
-        return part_copies(
-            early_sent, moved_part.at[0], move_part_sem, (0,), layer + 1
-        )[:half]
 
     def wait_edges(b):
         view = moved.at[b, :, :, pl.ds(0, len(edges) * cells)]
@@ -305,10 +318,11 @@
         pl.when(has_high)(ahead_low(b).wait_recv)
 
     def receive_whole(b):
-        wait_edges(b)
+        pl.when(even)(lambda: wait_edges(b))
         wait_middle(b)
         wait_rims(b)
         part_waits(moved_part.at[b], move_part_sem, (b,), 1)
+        hand_across(b + 1)
         coeff = coefficients(moved_part[b])
         pieces = [stacked(moved_rim[b, 0, 0], moved_rim[b, 0, 1])]
         pieces += [piece(moved.at[b], q) for q in range(count)]
@@ -331,7 +345,8 @@
         def gathered(q, chosen):
             return turned_dot(q, chosen, [pieces[shifted(q, s)] for s in chosen])
 
-        wait_edges(b)
+        hand_across(b)
+        pl.when(even)(lambda: wait_edges(b))
         pieces = {q: piece(moved.at[b], q) for q in edges}
         left_over = {}
         for q in range(count):
@@ -345,6 +360,7 @@
             if left_over[q]:
                 base[q] -= gathered(q, left_over[q])
         wait_rims(b)
+        hand_across(b + 1)
         part_waits(moved_part.at[b], move_part_sem, (b,), 1)
         coeff = coefficients(moved_part[b])
         fields = []
@@ -372,7 +388,7 @@
 
     def send_rims(b):
         pl.when(has_high)(ahead_high(b).start)
-        pl.when(has_low)(ahead_low(b).start)
+        pl.when(even & has_low)(ahead_low(b).start)
 
     def send_main(b):
         for copy in ahead_main(b):
@@ -383,7 +399,7 @@
         send_main(b)
 
     def send_parts(b, stacks):
-        moved_part_sent[b] = folded(stacks, right_next)
+        moved_part_sent[b, 0], moved_part_sent[b, 1] = folded(stacks, right_next)
         for copy in ahead_parts(b):
             copy.start()
 
@@ -394,17 +410,13 @@
                 send_field(b)
         stacks = [piece(sent.at[0], q) for q in range(count)]
         downs[0].wait_recv()
-        first_level = level_sums(stacks, right_next.at[0])
-        early_sent[...] = packed(
-            jnp.concatenate([first_level, jnp.zeros_like(first_level)], axis=1)
-        )
-        for copy in early_parts():
+        moved_part_sent[0, 0] = packed(level_sums(stacks, right_next.at[0]))
+        for copy in ahead_parts(0)[:half]:
             copy.start()
         if batches > 1:
             send_main(1)
         downs[1].wait_recv()
-        second_level = level_sums(stacks, right_next.at[1])
-        moved_part_sent[0] = packed(jnp.concatenate([first_level, second_level], axis=1))
+        moved_part_sent[0, 1] = packed(level_sums(stacks, right_next.at[1]))
         for copy in ahead_parts(0)[half:]:
             copy.start()
         if batches > 1:
@@ -426,8 +438,9 @@
                 for copy in downs:
                     copy.wait_recv()
             stacks = couple(b, receive(b, b == 0))
+            send_rims(b)
             send_parts(b, stacks)
-            send_field(b)
+            send_main(b)
 
     @pl.when(has_prev & jnp.logical_not(has_next))
     def _():
@@ -447,11 +460,13 @@
     def drained(ref, index):
         pltpu.make_async_copy(ref, ref, sent_sem.at[index]).wait()
 
+    pl.when(has_prev & odd)(lambda: drained(moved_rim.at[:, 1], 3))
+
     @pl.when(has_next)
     def _():
         drained(sent, 0)
         pl.when(has_high)(lambda: drained(moved_rim.at[:, 0], 1))
-        pl.when(has_low)(lambda: drained(moved_rim.at[:, 1], 2))
+        pl.when(even & has_low)(lambda: drained(moved_rim.at[:, 1], 2))
         for b in range(batches):
             part_waits(moved_part.at[b], move_part_sem, (b,), 0)
 
@@ -467,8 +482,8 @@
     dma = pltpu.SemaphoreType.DMA
 
     def fold_shape(size):
-        height = max(4 * size * rank // TILE, 1)
-        return (height, 4 * size * rank // height)
+        height = max(2 * size * rank // TILE, 1)
+        return (height, 2 * size * rank // height)
 
     return pl.pallas_call(
         functools.partial(kernel, layers, leafs, batches),
@@ -489,13 +504,12 @@
             pltpu.VMEM((count, 2 * group, cells), F32),
             pltpu.VMEM((2, 2, rows, cells), BF16),
             pltpu.VMEM((sources,) + fold_shape(rows), BF16),
-            pltpu.VMEM(fold_shape(rows), BF16),
+            pltpu.VMEM((2,) + fold_shape(rows), BF16),
             pltpu.VMEM((batches, 2, group, width), BF16),
             pltpu.VMEM((batches, 2, group, width), BF16),
             pltpu.VMEM((batches, 2, 2, group, cells), BF16),
             pltpu.VMEM((batches, sources) + fold_shape(group), BF16),
-            pltpu.VMEM((batches,) + fold_shape(group), BF16),
-            pltpu.VMEM(fold_shape(group), BF16),
+            pltpu.VMEM((batches, 2) + fold_shape(group), BF16),
             dma((6,)),
             dma((2, 2)),
             dma((2,)),
@@ -503,7 +517,7 @@
             dma((batches, 2)),
             dma((batches, 2)),
             dma((2, batches)),
-            dma((3,)),
+            dma((4,)),
             pltpu.SemaphoreType.REGULAR,
         ],
         compiler_params=pltpu.CompilerParams(collective_id=0, has_side_effects=True),

time: 23 us -> 22.3 us (0.970)
  Pallas kernels: 22.2 us -> 21.5 us
    pallas_call x1, Pallas kernels: 22.2 us -> 21.5 us  [body(): pl.pallas_call(functools.partial(kernel, layers, leafs, batches), out_sha...]
where the time goes in v5:
time: 22.3 us; the launch traced here: 22.2 us
  Pallas kernels  21.5 us (96%)
  local copies, waits for them, and re-layouts  0.66 us (3%)
    pallas_call x1, Pallas kernels, body(): pl.pallas_call(functools.partial(kernel, layers, leafs, batches), out_sha...  21.5 us
    unnamed x1, local copies, waits for them, and re-layouts  0.66 us

profile of v5, /device:TPU:25, one launch (start us, length us, event | category | flops | bytes accessed | tf_op | source)
XLA Modules:
  0.0 22.2 jit_solution(1958219131705353974)
XLA Ops:
  0.0 21.5 %shard_map.64 = bf16[1,2,32,1024]{3,2,1,0:T(8,128)(2,1)S(1)} custom-call(bf16[1,2,32,1024]{3,2,1,0:T(8,128)(2,1)} %source_hbm.1, bf16[1,3,2,1024,256]{4,3,2,1,0:T(8,128)(2,1)} %near_hbm.1, bf16[1,2,2,16,1024]{4,3,2,1,0:T(8,128)(2,1)} %right_hbm.1, bf16[1,2,2,16,1024]{4,3,2,1,0:T(8,128)(2,1)} %left_hbm.1, bf16[1,1024]{1,0:T(2,128)(2,1)} %coupling_hbm.1, ...), custom_call_target="tpu_custom_call" | custom-call | tf_op jit(solution)/shard_map/pallas_call | solution.py:488
  21.5 0.7 %copy.8 = bf16[1,2,32,1024]{3,2,1,0:T(8,128)(2,1)} copy(bf16[1,2,32,1024]{3,2,1,0:T(8,128)(2,1)S(1)} %shard_map.64) | data formatting | bytes 262144

commit v6 on v5

--- a/solution.py
+++ b/solution.py
@@ -129,25 +129,26 @@
             [total[at:at + height] for at in range(0, total.shape[0], height)], axis=1
         ).astype(BF16)
 
-    def part_copies(src, dst, sems, index, to_layer):
+    def part_copies(src, dst, send_sem, recv_sem, to_layer):
         copies = []
+
+        def part_copy(level, slot, to_leaf):
+            return pltpu.make_async_remote_copy(
+                src_ref=src.at[level], dst_ref=dst.at[slot], send_sem=send_sem, recv_sem=recv_sem,
+                device_id=(to_layer, to_leaf), device_id_type=pl.DeviceIdType.MESH,
+            )
+
         slot = lax.rem(leaf, half)
         for other in range(half):
-            copies.append(remote(
-                src.at[0], dst.at[slot], sems, index,
-                to_layer, (1 - upper) * half + other,
-            ))
+            copies.append(part_copy(0, slot, (1 - upper) * half + other))
         slot = half + lax.rem(leaf, quarter)
         sibling = lower + 1 - 2 * lax.rem(lower, 2)
         for other in range(quarter):
-            copies.append(remote(
-                src.at[1], dst.at[slot], sems, index,
-                to_layer, sibling * quarter + other,
-            ))
+            copies.append(part_copy(1, slot, sibling * quarter + other))
         return copies
 
-    def part_waits(dst, sems, index, way):
-        pltpu.make_async_copy(dst, dst, sems.at[(way,) + index]).wait()
+    def landed(view, sem):
+        pltpu.make_async_copy(view, view, sem).wait()
 
     def coefficients(parts):
         first = parts[0].astype(F32)
@@ -203,7 +204,7 @@
         source.at[:, :, block(count - 1)], rim.at[0], rim_sem, (0,), layer, leaf + 1
     )
     to_low = remote(source.at[:, :, block(0)], rim.at[1], rim_sem, (1,), layer, leaf - 1)
-    source_parts = part_copies(part_sent, part, part_sem, (), layer)
+    source_parts = part_copies(part_sent, part, part_sem.at[0], part_sem.at[1], layer)
 
     @pl.when(has_prev)
     def _():
@@ -240,7 +241,7 @@
         inner[:, :, block(q)] += plain_dot(q, s, stacked(rim[side, 0], rim[side, 1])).reshape(
             2, rows, cells
         )
-    part_waits(part, part_sem, (), 1)
+    landed(part, part_sem.at[1])
     coeff = coefficients(part)
     for q in range(count):
         inner[:, :, block(q)] += far_leaf(q, coeff).reshape(2, rows, cells)
@@ -273,7 +274,7 @@
     def rim_copy(source_ref, q, b, side, to_layer, to_leaf):
         return pltpu.make_async_remote_copy(
             src_ref=source_ref.at[b, :, :, block(q)], dst_ref=moved_rim.at[b, side],
-            send_sem=sent_sem.at[1 + side], recv_sem=move_rim_sem.at[b, side],
+            send_sem=sent_sem.at[1 + side], recv_sem=move_rim_sem.at[b],
             device_id=(to_layer, to_leaf), device_id_type=pl.DeviceIdType.MESH,
         )
 
@@ -286,7 +287,7 @@
     def across_low(b):
         return pltpu.make_async_remote_copy(
             src_ref=moved.at[b, :, :, block(0)], dst_ref=moved_rim.at[b, 1],
-            send_sem=sent_sem.at[3], recv_sem=move_rim_sem.at[b, 1],
+            send_sem=sent_sem.at[3], recv_sem=move_rim_sem.at[b],
             device_id=(layer, leaf - 1), device_id_type=pl.DeviceIdType.MESH,
         )
 
@@ -300,7 +301,7 @@
 
     def ahead_parts(b):
         return part_copies(
-            moved_part_sent.at[b], moved_part.at[b], move_part_sem, (b,), layer + 1
+            moved_part_sent.at[b], moved_part.at[b], sent_sem.at[4], move_part_sem.at[b], layer + 1
         )
 
 
@@ -314,14 +315,16 @@
             pltpu.make_async_copy(view, view, move_sem.at[b, 1]).wait()
 
     def wait_rims(b):
-        pl.when(has_low)(ahead_high(b).wait_recv)
-        pl.when(has_high)(ahead_low(b).wait_recv)
+        sem = move_rim_sem.at[b]
+        pl.when(has_low & has_high)(lambda: landed(moved_rim.at[b], sem))
+        pl.when(jnp.logical_not(has_high))(lambda: landed(moved_rim.at[b, 0], sem))
+        pl.when(jnp.logical_not(has_low))(lambda: landed(moved_rim.at[b, 1], sem))
 
     def receive_whole(b):
         pl.when(even)(lambda: wait_edges(b))
         wait_middle(b)
         wait_rims(b)
-        part_waits(moved_part.at[b], move_part_sem, (b,), 1)
+        landed(moved_part.at[b], move_part_sem.at[b])
         hand_across(b + 1)
         coeff = coefficients(moved_part[b])
         pieces = [stacked(moved_rim[b, 0, 0], moved_rim[b, 0, 1])]
@@ -361,7 +364,7 @@
                 base[q] -= gathered(q, left_over[q])
         wait_rims(b)
         hand_across(b + 1)
-        part_waits(moved_part.at[b], move_part_sem, (b,), 1)
+        landed(moved_part.at[b], move_part_sem.at[b])
         coeff = coefficients(moved_part[b])
         fields = []
         for q in range(count):
@@ -414,12 +417,15 @@
         for copy in ahead_parts(0)[:half]:
             copy.start()
         if batches > 1:
-            send_main(1)
+            for copy in ahead_main(1)[:len(edges)]:
+                copy.start()
         downs[1].wait_recv()
         moved_part_sent[0, 1] = packed(level_sums(stacks, right_next.at[1]))
         for copy in ahead_parts(0)[half:]:
             copy.start()
         if batches > 1:
+            for copy in ahead_main(1)[len(edges):]:
+                copy.start()
             send_rims(1)
         for b in range(1, batches):
             send_parts(b, [piece(sent.at[b], q) for q in range(count)])
@@ -449,7 +455,7 @@
 
     pl.when(has_high)(to_high.wait_send)
     pl.when(has_low)(to_low.wait_send)
-    part_waits(part, part_sem, (), 0)
+    landed(part, part_sem.at[0])
 
     @pl.when(has_prev)
     def _():
@@ -467,8 +473,7 @@
         drained(sent, 0)
         pl.when(has_high)(lambda: drained(moved_rim.at[:, 0], 1))
         pl.when(even & has_low)(lambda: drained(moved_rim.at[:, 1], 2))
-        for b in range(batches):
-            part_waits(moved_part.at[b], move_part_sem, (b,), 0)
+        drained(moved_part, 4)
 
 
 def body(layers, leafs, right_side, near_blocks, right_bases, left_bases, coupling, ranks):
@@ -515,9 +520,9 @@
             dma((2,)),
             dma((2, 2)),
             dma((batches, 2)),
-            dma((batches, 2)),
-            dma((2, batches)),
-            dma((4,)),
+            dma((batches,)),
+            dma((batches,)),
+            dma((5,)),
             pltpu.SemaphoreType.REGULAR,
         ],
         compiler_params=pltpu.CompilerParams(collective_id=0, has_side_effects=True),

time: 22.3 us -> 22.3 us (level)
  no operation moved by 1% of the time
where the time goes in v6:
time: 22.3 us; the launch traced here: 22.1 us
  Pallas kernels  21.4 us (96%)
  local copies, waits for them, and re-layouts  0.66 us (3%)
    pallas_call x1, Pallas kernels, body(): pl.pallas_call(functools.partial(kernel, layers, leafs, batches), out_sha...  21.4 us
    unnamed x1, local copies, waits for them, and re-layouts  0.66 us

profile of v6, /device:TPU:25, one launch (start us, length us, event | category | flops | bytes accessed | tf_op | source)
XLA Modules:
  0.0 22.1 jit_solution(4256919518869488892)
XLA Ops:
  0.0 21.4 %shard_map.64 = bf16[1,2,32,1024]{3,2,1,0:T(8,128)(2,1)S(1)} custom-call(bf16[1,2,32,1024]{3,2,1,0:T(8,128)(2,1)} %source_hbm.1, bf16[1,3,2,1024,256]{4,3,2,1,0:T(8,128)(2,1)} %near_hbm.1, bf16[1,2,2,16,1024]{4,3,2,1,0:T(8,128)(2,1)} %right_hbm.1, bf16[1,2,2,16,1024]{4,3,2,1,0:T(8,128)(2,1)} %left_hbm.1, bf16[1,1024]{1,0:T(2,128)(2,1)} %coupling_hbm.1, ...), custom_call_target="tpu_custom_call" | custom-call | tf_op jit(solution)/shard_map/pallas_call | solution.py:493
  21.5 0.7 %copy.8 = bf16[1,2,32,1024]{3,2,1,0:T(8,128)(2,1)} copy(bf16[1,2,32,1024]{3,2,1,0:T(8,128)(2,1)S(1)} %shard_map.64) | data formatting | bytes 262144

commit v7 on v6

--- a/solution.py
+++ b/solution.py
@@ -254,6 +254,15 @@
                     near_turned[q, pl.ds((2 * s + c) * cells, cells), :] = near[q, s, c].T
 
     pl.when(has_next)(lambda: pl.semaphore_wait(ready_sem, 1))
+
+    pl.when(has_high)(to_high.wait_send)
+    pl.when(has_low)(to_low.wait_send)
+    landed(part, part_sem.at[0])
+
+    @pl.when(has_prev)
+    def _():
+        for copy in downs:
+            copy.wait_send()
 
     def rows_of(b):
         return pl.ds(b * group, group)
@@ -452,16 +461,6 @@
     def _():
         for b in range(batches):
             receive(b, b == 0)
-
-    pl.when(has_high)(to_high.wait_send)
-    pl.when(has_low)(to_low.wait_send)
-    landed(part, part_sem.at[0])
-
-    @pl.when(has_prev)
-    def _():
-        for copy in downs:
-            copy.wait_send()
-
 
     def drained(ref, index):
         pltpu.make_async_copy(ref, ref, sent_sem.at[index]).wait()

time: 22.3 us -> 22.3 us (level)
  no operation moved by 1% of the time
where the time goes in v7:
time: 22.3 us; the launch traced here: 22.1 us
  Pallas kernels  21.4 us (96%)
  local copies, waits for them, and re-layouts  0.66 us (3%)
    pallas_call x1, Pallas kernels, body(): pl.pallas_call(functools.partial(kernel, layers, leafs, batches), out_sha...  21.4 us
    unnamed x1, local copies, waits for them, and re-layouts  0.66 us

profile of v7, /device:TPU:25, one launch (start us, length us, event | category | flops | bytes accessed | tf_op | source)
XLA Modules:
  0.0 22.1 jit_solution(11847166428482679880)
XLA Ops:
  0.0 21.4 %shard_map.64 = bf16[1,2,32,1024]{3,2,1,0:T(8,128)(2,1)S(1)} custom-call(bf16[1,2,32,1024]{3,2,1,0:T(8,128)(2,1)} %source_hbm.1, bf16[1,3,2,1024,256]{4,3,2,1,0:T(8,128)(2,1)} %near_hbm.1, bf16[1,2,2,16,1024]{4,3,2,1,0:T(8,128)(2,1)} %right_hbm.1, bf16[1,2,2,16,1024]{4,3,2,1,0:T(8,128)(2,1)} %left_hbm.1, bf16[1,1024]{1,0:T(2,128)(2,1)} %coupling_hbm.1, ...), custom_call_target="tpu_custom_call" | custom-call | tf_op jit(solution)/shard_map/pallas_call | solution.py:492
  21.4 0.7 %copy.8 = bf16[1,2,32,1024]{3,2,1,0:T(8,128)(2,1)} copy(bf16[1,2,32,1024]{3,2,1,0:T(8,128)(2,1)S(1)} %shard_map.64) | data formatting | bytes 262144
